TPU v7x, 32 devices: a whole 2x2x4 slice. The times are simulated.
32 devices in a mesh: sub: 4 (over y, x), elem: 8 (over z, core).
Axes of the slice: x: 2, y: 2, z: 4, core: 2. Of those that a mesh axis runs over, the one named last changes fastest.
Arguments:
- element_tiles: bfloat16 [256, 128, 128], P(('sub', 'elem')), parts along dimension 0, may hold values from -0.5 to 0.5
- element_blocks: int32 [256, 2], P(('sub', 'elem')), parts along dimension 0, may hold values from 0 to 31
- mode_shapes: bfloat16 [16384, 1024], P(('sub', 'elem')), parts along dimension 0, may hold values from -0.5 to 0.5
- trial_modes: bfloat16 [4096, 128], P('sub'), parts along dimension 0, may hold values from -0.1875 to 0.1875
Outputs:
- reduced_stiffness: float32 [4096, 1024], P(('sub', 'elem')), parts along dimension 0
- interface_forces: float32 [4096, 128], P(('sub', 'elem')), parts along dimension 0
There are 4 independent parts, one for each index of `sub`. A program takes and returns all parts, laid end to end along the dimension named above; each array names one. Nothing has to cross between parts.
Inputs may be any that keep to these rules, and one draw needn't show every extreme that they name: `element_blocks`: each row gives the row block and the column block of one element tile.
All inputs are finite; a program needn't handle non-finite values.
Results may differ from a plain program's by a relative error of at most 0.0029.
Values may be sent and summed in bfloat16 or wider, within the bound.
No kernel may reach another device: no remote copies, remote signals or barrier semaphores. Data moves between devices by JAX's collectives and lax.ppermute only.
A program may use at most 64 MiB of HBM per device.

v0:
```python
import functools

import jax
import jax.numpy as jnp
from jax import lax
from jax.experimental import pallas as pl
from jax.experimental.pallas import tpu as pltpu
from jax.sharding import PartitionSpec as P


AXES = ("sub", "elem")
LANES, BELOW = 128, 8
FLIPS = (1, 2, 1, 2)
CHUNKS = len(FLIPS)
SPARE = 2 << 20
SMEM = pl.BlockSpec(memory_space=pltpu.SMEM)
VMEM = pl.BlockSpec(memory_space=pltpu.VMEM)
ANY = pl.BlockSpec(memory_space=pl.ANY)
HBM = pl.BlockSpec(memory_space=pltpu.HBM)


class Plan:
    def __init__(self, mesh):
        self.parts, self.places = mesh.shape["sub"], mesh.shape["elem"]
        self.chips = self.places // 2
        self.root = self.chips // 2 - 1
        self.beyond = self.root + 1
        self.paired = self.parts % 4 == 0

    def kind(self, part):
        return (part ^ (part >> 1)) & 1 if self.paired else part * 0

    def device(self, part, step, core):
        chip = self.chips - 1 - step if self.kind(part) else step
        return part * self.places + chip * 2 + core

    def beside(self, part, step, core, flip):
        return self.device(part, step, core) + ((part ^ flip) - part) * self.places

    def pairs(self, route):
        return [route(part, core) for part in range(self.parts) for core in range(2)]

    def to_root(self, step):
        return self.pairs(lambda p, c: (self.device(p, step, c), self.device(p, self.root, c)))

    def aside(self, step, flip):
        return self.pairs(lambda p, c: (self.device(p, step, c), self.beside(p, step, c, flip)))

    def aside_to_root(self, step, flip):
        return self.pairs(lambda p, c: (self.beside(p, step, c, flip), self.device(p, self.root, c)))

    def swap(self):
        return self.pairs(lambda p, c: (self.device(p, self.root, c), self.device(p, self.root, 1 - c)))

    def from_root(self, step, cross):
        return self.pairs(lambda p, c: (self.device(p, self.root, c), self.device(p, step, c ^ cross)))


def tiles_kernel(t_ref, b_ref, out_ref, low_ref):
    local, width, _ = t_ref.shape
    for t in range(local):
        out_ref[t * width : (t + 1) * width, :] = t_ref[t]
    low_ref[...] = jnp.zeros_like(low_ref)
    low_ref[: b_ref.shape[0], :local] = b_ref[...]
    out_ref[local * width :, :] = low_ref[...].astype(jnp.float32).astype(out_ref.dtype)


def join_kernel(*refs):
    parts, all_ref = refs[:-1], refs[-1]
    row = 0
    for part in parts:
        all_ref[row : row + part.shape[0], :] = part[...]
        row += part.shape[0]


def root_kernel(plan, spans, width, modes, elems, where_ref, *refs):
    chips, n, half, below = plan.chips, len(refs) - 2 * plan.chips - 9, modes // 2, BELOW
    p_in, outs = refs[:n], refs[n : n + 2 * chips]
    p_all, t_all, low_idx, vec_idx, idx, q_sum, q_low, k_acc, sems = refs[n + 2 * chips :]
    kind, core = where_ref[0], where_ref[1]
    depth, local = p_all.shape[0] // plan.places, elems // plan.places
    per = depth // width
    mine = pl.ds(pl.multiple_of(core * half, half), half)
    rest = pl.ds(pl.multiple_of((1 - core) * half, half), half)

    first, second, numbers = [], [], []

    def copy(src, to):
        at = len(first) + len(second) + len(numbers)
        return pltpu.make_async_copy(src, to, sems.at[at])

    for slot, (p_at, t_at, low) in enumerate(spans):
        p_ref, t_ref = p_in[p_at], p_in[t_at]
        to = pl.ds(slot * depth, depth)
        numbers.append(
            copy(t_ref.at[pl.ds(low + local * width, below), :], low_idx.at[pl.ds(slot * below, below), :])
        )
        for j in range(local // per):
            block = t_ref.at[pl.ds(low + j * depth, depth), :]
            first.append(copy(block, t_all.at[to, pl.ds(j * width, width)]))
        first.append(copy(p_ref.at[:, mine], p_all.at[to, mine]))
        second.append(copy(p_ref.at[:, rest], p_all.at[to, rest]))
    for c in numbers + first + second:
        c.start()
    for c in numbers:
        c.wait()
    vec_idx[...] = low_idx[...].astype(jnp.float32).astype(jnp.int32)
    to_smem = copy(vec_idx, idx)
    to_smem.start()
    q_sum[...] = jnp.zeros_like(q_sum)
    to_smem.wait()
    for c in first:
        c.wait()

    def row_of(block):
        place, b = block // per, block % per
        chip, other = place // 2, (place % 2) ^ core
        step = jnp.where(kind == 1, chips - 1 - chip, chip)
        return pl.ds(pl.multiple_of(((step * 2 + other) * per + b) * width, width), width)

    def element(e, carry):
        slot, t = e // local, e % local
        tile = t_all[
            pl.ds(pl.multiple_of(slot * depth + t % per * width, width), width),
            pl.ds(pl.multiple_of(t // per * width, width), width),
        ]
        r, c = idx[slot * below, t], idx[slot * below + 1, t]
        stiff = jnp.dot(tile, p_all[row_of(c), mine], preferred_element_type=jnp.float32).astype(jnp.bfloat16)
        q_sum[row_of(r), :] += stiff.astype(jnp.float32)
        return carry

    lax.fori_loop(0, elems, element, 0, unroll=64)
    for c in second:
        c.wait()
    chunk = p_all.shape[0] // 4
    for i in range(4):
        rows = pl.ds(i * chunk, chunk)
        q_low[rows, :] = q_sum[rows, :].astype(jnp.bfloat16)
        part = lax.dot_general(
            p_all[rows, :], q_low[rows, :], (((0,), (0,)), ((), ())), preferred_element_type=jnp.float32
        )
        if i == 0:
            k_acc[...] = part
        else:
            k_acc[...] += part
    strip = modes // plan.places
    for step in range(chips):
        chip = jnp.where(kind == 1, chips - 1 - step, step)
        for cross in range(2):
            row = pl.multiple_of((chip * 2 + (core ^ cross)) * strip, strip)
            outs[2 * step + cross][...] = k_acc[pl.ds(row, strip), :].astype(jnp.bfloat16)


def final_kernel(n, where_ref, trial_ref, *refs):
    same, cross = refs[:n], refs[n : 2 * n]
    k_ref, f_ref, rows = refs[2 * n :]
    core, step = where_ref[1], where_ref[2]
    half = same[0].shape[1]
    mine = pl.ds(pl.multiple_of(core * half, half), half)
    other = pl.ds(pl.multiple_of((1 - core) * half, half), half)
    for i in range(n):

        @pl.when(step == i)
        def _():
            rows[:, mine] = same[i][...]
            rows[:, other] = cross[i][...]

    k = rows[...]
    k_ref[...] = k.astype(jnp.float32)
    f_ref[...] = jnp.dot(k, trial_ref[...], preferred_element_type=jnp.float32)


def body(plan, element_tiles, element_blocks, mode_shapes, trial_modes):
    part, place = lax.axis_index("sub"), lax.axis_index("elem")
    kind, core, chip = plan.kind(part), place % 2, place // 2
    step = jnp.where(kind == 1, plan.chips - 1 - chip, chip)
    where = jnp.stack([kind, core, step]).astype(jnp.int32)
    local, width, _ = element_tiles.shape
    depth, modes = mode_shapes.shape
    root, chips, beyond = plan.root, plan.chips, plan.beyond
    per = depth // width
    wide = modes + local // per * width
    total, elems = depth * plan.places, local * plan.places
    strip, half = modes // plan.places, modes // 2

    def send(x, pairs):
        return lax.ppermute(x, AXES, pairs)

    def kernel(fn, out, ins, scratch, limit, flops=0):
        return pl.pallas_call(
            fn,
            out_shape=out,
            in_specs=ins,
            out_specs=[VMEM] * len(out),
            scratch_shapes=scratch,
            compiler_params=pltpu.CompilerParams(vmem_limit_bytes=limit + SPARE),
            cost_estimate=pl.CostEstimate(flops=flops, bytes_accessed=0, transcendentals=0),
        )

    def array(shape, dtype=jnp.bfloat16):
        return jax.ShapeDtypeStruct(shape, dtype)

    def joined(parts):
        rows, columns = sum(x.shape[0] for x in parts), parts[0].shape[1]
        [whole] = kernel(join_kernel, [array((rows, columns))], [VMEM] * len(parts), [], 6 * rows * columns)(*parts)
        return whole

    chunk = depth // CHUNKS
    sides, got = [], {}
    if plan.paired:
        sides = [send(mode_shapes[i * chunk : (i + 1) * chunk], plan.aside(beyond, FLIPS[i])) for i in range(CHUNKS)]
    for s in range(chips - 1, -1, -1):
        if s != root and not (s == beyond and plan.paired):
            got[s] = [send(mode_shapes, plan.to_root(s))]
    if plan.paired:
        got[beyond] = [send(x, plan.aside_to_root(beyond, FLIPS[i])) for i, x in enumerate(sides)]
    [tiles] = kernel(
        tiles_kernel,
        [array((local * width + BELOW, width))],
        [VMEM, VMEM],
        [pltpu.VMEM((BELOW, width), jnp.int32)],
        4 * local * width * width,
    )(element_tiles, element_blocks.T)
    got[root] = [mode_shapes]
    there = {s: tiles if s == root else send(tiles, plan.to_root(s)) for s in range(chips - 1, -1, -1)}
    late = [beyond] if plan.paired else []
    early = [s for s in range(chips) if s not in late]
    p_in, place = [], {}

    def hold(x, keys):
        for core, y in enumerate((x, send(x, plan.swap()))):
            for i, key in enumerate(keys):
                place[(*key, core)] = (len(p_in), i * (local * width + BELOW))
            p_in.append(y)

    for s in range(chips):
        hold(got[s][0] if len(got[s]) == 1 else joined(got[s]), [("p", s)])
    hold(joined([there[s] for s in early]), [("t", s) for s in early])
    for s in late:
        hold(there[s], [("t", s)])
    spans = [(place["p", s, c][0], *place["t", s, c]) for s in range(chips) for c in range(2)]

    pieces = kernel(
        functools.partial(root_kernel, plan, spans, width, modes, elems),
        [array((strip, half))] * plan.places,
        [SMEM] + [ANY] * len(p_in),
        [
            pltpu.VMEM((total, modes), jnp.bfloat16),
            pltpu.VMEM((total, wide - modes), jnp.bfloat16),
            pltpu.VMEM((plan.places * BELOW, LANES), jnp.bfloat16),
            pltpu.VMEM((plan.places * BELOW, LANES), jnp.int32),
            pltpu.SMEM((plan.places * BELOW, LANES), jnp.int32),
            pltpu.VMEM((total, half), jnp.float32),
            pltpu.VMEM((total, half), jnp.bfloat16),
            pltpu.VMEM((modes, half), jnp.float32),
            pltpu.SemaphoreType.DMA((plan.places * (local // per + 3) + 1,)),
        ],
        total * (wide + 3 * half) * 2 + 4 * modes * half,
        2 * elems * width * width * half + 2 * total * modes * half,
    )(where, *p_in)
    same = [pieces[2 * s] if s == root else send(pieces[2 * s], plan.from_root(s, 0)) for s in range(chips)]
    cross = [send(pieces[2 * s + 1], plan.from_root(s, 1)) for s in range(chips)]
    return kernel(
        functools.partial(final_kernel, chips),
        [array((strip, modes), jnp.float32), array((strip, trial_modes.shape[1]), jnp.float32)],
        [SMEM] + [VMEM] * (2 * chips + 1),
        [pltpu.VMEM((strip, modes), jnp.bfloat16)],
        4 << 20,
    )(where, trial_modes, *same, *cross)


def solution(mesh):
    plan = Plan(mesh)
    in_specs = (
        P(AXES, None, None),
        P(AXES, None),
        P(AXES, None),
        P("sub", None),
    )
    out_specs = (P(AXES, None), P(AXES, None))

    def step(*args):
        return body(plan, *args)

    return jax.shard_map(step, mesh=mesh, in_specs=in_specs, out_specs=out_specs, check_vma=False)
```

profile of v0, /device:TPU:3, one launch (start us, length us, event | category | flops | bytes accessed | tf_op | source)
XLA Modules:
  0.0 101.0 jit_solution(13905861720541557427)
XLA Ops:
  0.6 0.0 copy-start
  0.6 0.0 copy-start.2
  0.6 1.4 %fusion = (bf16[128,1024]{1,0:T(8,128)(2,1)S(1)}, bf16[128,1024]{1,0:T(8,128)(2,1)S(1)}, bf16[128,1024]{1,0:T(8,128)(2,1)S(1)}, bf16[128,1024]{1,0:T(8,128)(2,1)S(1)}) fusion(bf16[512,1024]{1,0:T(8,128)(2,1)} %refs_2_.1), kind=kLoop, calls=%fused_computation.1 | loop fusion | bytes 2097152 | tf_op jit(solution)/shard_map/slice | solution.py:211
  2.0 0.7 collective-permute-start.9
  2.7 0.7 collective-permute-start.7
  3.4 0.0 copy-done
  3.4 1.7 %collective-permute-start = (bf16[512,1024]{1,0:T(8,128)(2,1)S(1)}, bf16[512,1024]{1,0:T(8,128)(2,1)}, u32[]{:S(2)}, u32[]{:S(2)}) collective-permute-start(bf16[512,1024]{1,0:T(8,128)(2,1)S(1)} %copy-done), channel_id=1, source_target_pairs={{0,2},{1,3},{14,12},{15,13},{22,20},{23,21},{24,26},{25,27}} | collective-permute-start | bytes 3145736 | tf_op jit(solution)/shard_map/ppermute | solution.py:187
  5.1 6.1 %collective-permute-start.12 = (bf16[512,1024]{1,0:T(8,128)(2,1)S(1)}, bf16[512,1024]{1,0:T(8,128)(2,1)}, u32[]{:S(2)}, u32[]{:S(2)}) collective-permute-start(bf16[512,1024]{1,0:T(8,128)(2,1)S(1)} %copy-done), channel_id=1, source_target_pairs={{6,2},{7,3},{8,12},{9,13},{16,20},{17,21},{30,26},{31,27}} | collective-permute-start | bytes 3145736 | tf_op jit(solution)/shard_map/ppermute | solution.py:187
  11.2 0.8 collective-permute-start.5
  12.0 0.0 copy-done.2
  12.0 0.0 copy-done.3
  12.0 0.0 collective-permute-done.9
  12.1 0.7 collective-permute-start.17
  12.7 0.0 collective-permute-done.7
  12.8 0.7 collective-permute-start.3
  13.4 0.0 collective-permute-done.5
  13.5 0.7 collective-permute-start.10
  14.1 0.0 collective-permute-done.3
  14.1 0.7 collective-permute-start.8
  14.8 0.0 collective-permute-done.17.refs_10_
  14.8 0.7 collective-permute-start.6
  15.5 0.0 collective-permute-done.10.refs_3_
  15.5 0.7 collective-permute-start.4
  16.2 0.0 collective-permute-done.8.refs_2_
  16.2 33.7 %collective-permute-start.15 = (bf16[1032,128]{1,0:T(8,128)(2,1)S(1)}, bf16[1032,128]{1,0:T(8,128)(2,1)S(1)}, u32[]{:S(2)}, u32[]{:S(2)}) collective-permute-start(bf16[1032,128]{1,0:T(8,128)(2,1)S(1)} %shard_map.60.refs_1_), channel_id=1, source_target_pairs={{6,2},{7,3},{8,12},{9,13},{16,20},{17,21},{30,26},{31,27}} | collective-permute-start | bytes 792584 | tf_op jit(solution)/shard_map/ppermute | solution.py:187
  50.0 0.0 collective-permute-done.6.refs_1_
  50.0 0.7 collective-permute-start.14
  50.7 0.0 collective-permute-done.4.refs_0_
  50.7 0.7 collective-permute-start.18
  51.4 0.1 shard_map.59.refs_4_
  51.4 3.2 %collective-permute-done.15.refs_2_ = bf16[1032,128]{1,0:T(8,128)(2,1)S(1)} collective-permute-done((bf16[1032,128]{1,0:T(8,128)(2,1)S(1)}, bf16[1032,128]{1,0:T(8,128)(2,1)S(1)}, u32[]{:S(2)}, u32[]{:S(2)}) %collective-permute-start.15) | collective-permute-done | bytes 264224 | tf_op jit(solution)/shard_map/ppermute | solution.py:187
  54.6 1.7 %collective-permute-start.2 = (bf16[512,1024]{1,0:T(8,128)(2,1)S(1)}, bf16[512,1024]{1,0:T(8,128)(2,1)}, u32[]{:S(2)}, u32[]{:S(2)}) collective-permute-start(bf16[512,1024]{1,0:T(8,128)(2,1)S(1)} %copy-done), channel_id=1, source_target_pairs={{2,3},{3,2},{12,13},{13,12},{20,21},{21,20},{26,27},{27,26}} | collective-permute-start | bytes 3145736 | tf_op jit(solution)/shard_map/ppermute | solution.py:187
  56.2 0.0 collective-permute-done.14.refs_0_
  56.2 1.6 %collective-permute-start.11 = (bf16[512,1024]{1,0:T(8,128)(2,1)S(1)}, bf16[512,1024]{1,0:T(8,128)(2,1)}, u32[]{:S(2)}, u32[]{:S(2)}) collective-permute-start(bf16[512,1024]{1,0:T(8,128)(2,1)S(1)} %shard_map.59.refs_4_), channel_id=1, source_target_pairs={{2,3},{3,2},{12,13},{13,12},{20,21},{21,20},{26,27},{27,26}} | collective-permute-start | bytes 3145736 | tf_op jit(solution)/shard_map/ppermute | solution.py:187
  57.9 0.0 collective-permute-done.refs_0_
  57.9 1.6 %collective-permute-start.1 = (bf16[512,1024]{1,0:T(8,128)(2,1)}, bf16[512,1024]{1,0:T(8,128)(2,1)}, u32[]{:S(2)}, u32[]{:S(2)}) collective-permute-start(bf16[512,1024]{1,0:T(8,128)(2,1)} %collective-permute-done.refs_0_), channel_id=1, source_target_pairs={{2,3},{3,2},{12,13},{13,12},{20,21},{21,20},{26,27},{27,26}} | collective-permute-start | bytes 3145736 | tf_op jit(solution)/shard_map/ppermute | solution.py:187
  59.5 0.0 collective-permute-done.12.refs_6_
  59.5 1.6 %collective-permute-start.13 = (bf16[512,1024]{1,0:T(8,128)(2,1)}, bf16[512,1024]{1,0:T(8,128)(2,1)}, u32[]{:S(2)}, u32[]{:S(2)}) collective-permute-start(bf16[512,1024]{1,0:T(8,128)(2,1)} %collective-permute-done.12.refs_6_), channel_id=1, source_target_pairs={{2,3},{3,2},{12,13},{13,12},{20,21},{21,20},{26,27},{27,26}} | collective-permute-start | bytes 3145736 | tf_op jit(solution)/shard_map/ppermute | solution.py:187
  61.1 0.1 shard_map.61.refs_8_
  61.2 0.0 collective-permute-done.18.refs_11_
  61.2 1.6 %collective-permute-start.16 = (bf16[3096,128]{1,0:T(8,128)(2,1)S(1)}, bf16[3096,128]{1,0:T(8,128)(2,1)}, u32[]{:S(2)}, u32[]{:S(2)}) collective-permute-start(bf16[3096,128]{1,0:T(8,128)(2,1)S(1)} %shard_map.61.refs_8_), channel_id=1, source_target_pairs={{2,3},{3,2},{12,13},{13,12},{20,21},{21,20},{26,27},{27,26}} | collective-permute-start | bytes 2377736 | tf_op jit(solution)/shard_map/ppermute | solution.py:187
  62.8 0.1 pad_add_fusion.where_ref
  62.8 0.0 collective-permute-done.2.refs_3_
  62.9 0.0 collective-permute-done.16.refs_9_
  62.9 0.0 collective-permute-done.11.refs_5_
  62.9 0.0 collective-permute-done.1.refs_1_
  62.9 0.0 collective-permute-done.13.refs_7_
  62.9 10.5 %shard_map.62 = (bf16[128,512]{1,0:T(8,128)(2,1)S(1)}, bf16[128,512]{1,0:T(8,128)(2,1)S(1)}, bf16[128,512]{1,0:T(8,128)(2,1)S(1)}, bf16[128,512]{1,0:T(8,128)(2,...) custom-call(s32[3]{0:T(128)S(1)} %pad_add_fusion.where_ref, ...), custom_call_target="tpu_custom_call" | custom-call | flops 5368709120 | tf_op jit(solution)/shard_map/pallas_call | solution.py:243
  73.4 0.7 collective-permute-start.19
  74.1 0.7 collective-permute-start.20
  74.7 1.3 %collective-permute-start.21 = (bf16[128,512]{1,0:T(8,128)(2,1)S(1)}, bf16[128,512]{1,0:T(8,128)(2,1)S(1)}, u32[]{:S(2)}, u32[]{:S(2)}) collective-permute-start(bf16[128,512]{1,0:T(8,128)(2,1)S(1)} %get-tuple-element.13), channel_id=1, source_target_pairs={{2,6},{3,7},{12,8},{13,9},{20,16},{21,17},{26,30},{27,31}} | collective-permute-start | bytes 393224 | tf_op jit(solution)/shard_map/ppermute | solution.py:187
  76.0 0.7 collective-permute-start.22
  76.7 0.7 collective-permute-start.23
  77.4 0.0 collective-permute-done.19.refs_0_
  77.4 0.7 collective-permute-start.24
  78.1 0.0 collective-permute-done.20.refs_2_
  78.1 1.3 %collective-permute-start.25 = (bf16[128,512]{1,0:T(8,128)(2,1)S(1)}, bf16[128,512]{1,0:T(8,128)(2,1)S(1)}, u32[]{:S(2)}, u32[]{:S(2)}) collective-permute-start(bf16[128,512]{1,0:T(8,128)(2,1)S(1)} %get-tuple-element.17), channel_id=1, source_target_pairs={{2,7},{3,6},{12,9},{13,8},{20,17},{21,16},{26,31},{27,30}} | collective-permute-start | bytes 393224 | tf_op jit(solution)/shard_map/ppermute | solution.py:187
  79.4 14.5 %collective-permute-done.21.refs_3_ = bf16[128,512]{1,0:T(8,128)(2,1)S(1)} collective-permute-done((bf16[128,512]{1,0:T(8,128)(2,1)S(1)}, bf16[128,512]{1,0:T(8,128)(2,1)S(1)}, u32[]{:S(2)}, u32[]{:S(2)}) %collective-permute-start.21) | collective-permute-done | bytes 131104 | tf_op jit(solution)/shard_map/ppermute | solution.py:187
  93.9 0.0 collective-permute-done.22.refs_4_
  93.9 0.0 collective-permute-done.23.refs_5_
  93.9 0.0 collective-permute-done.24.refs_6_
  93.9 5.6 %collective-permute-done.25.refs_7_ = bf16[128,512]{1,0:T(8,128)(2,1)S(1)} collective-permute-done((bf16[128,512]{1,0:T(8,128)(2,1)S(1)}, bf16[128,512]{1,0:T(8,128)(2,1)S(1)}, u32[]{:S(2)}, u32[]{:S(2)}) %collective-permute-start.25) | collective-permute-done | bytes 131104 | tf_op jit(solution)/shard_map/ppermute | solution.py:187
  99.6 0.0 copy-done.1
  99.6 1.4 %shard_map.63 = (f32[128,1024]{1,0:T(8,128)}, f32[128,128]{1,0:T(8,128)}) custom-call(s32[3]{0:T(128)S(1)} %pad_add_fusion.where_ref, bf16[1024,128]{1,0:T(8,128)(2,1)S(1)} %copy-done.1, bf16[128,512]{1,0:T(8,128)(2,1)S(1)} %collective-permute-done.19.refs_0_, bf16[128,512]{1,0:T(8,128)(2,1)S(1)} %get-tuple-element.11.refs_1_, ...), custom_call_target="tpu_custom_call" | custom-call | tf_op jit(solution)/shard_map/pallas_call | solution.py:263
  (3 shorter events, 0.0 us)
Async XLA Ops:
  0.6 2.8 %copy-start = (bf16[512,1024]{1,0:T(8,128)(2,1)S(1)}, bf16[512,1024]{1,0:T(8,128)(2,1)}, u32[]{:S(2)}) copy-start(bf16[512,1024]{1,0:T(8,128)(2,1)} %refs_2_.1) | copy-start | bytes 3145732
  0.6 11.4 %copy-start.2 = (bf16[8,128,128]{2,1,0:T(8,128)(2,1)S(1)}, bf16[8,128,128]{2,1,0:T(8,128)(2,1)}, u32[]{:S(2)}) copy-start(bf16[8,128,128]{2,1,0:T(8,128)(2,1)} %t_ref.1) | copy-start | bytes 786436
  2.0 10.0 %collective-permute-start.9 = (bf16[128,1024]{1,0:T(8,128)(2,1)S(1)}, bf16[128,1024]{1,0:T(8,128)(2,1)S(1)}, u32[]{:S(2)}, u32[]{:S(2)}) collective-permute-start(bf16[128,1024]{1,0:T(8,128)(2,1)S(1)} %get-tuple-element.18), channel_id=1, source_target_pairs={{4,20},{5,21},{10,26},{11,27},{18,2},{19,3},{28,12},{29,13}} | collective-permute-start | bytes 786440 | tf_op jit(solution)/shard_map/ppermute | solution.py:187
  2.7 10.0 %collective-permute-start.7 = (bf16[128,1024]{1,0:T(8,128)(2,1)S(1)}, bf16[128,1024]{1,0:T(8,128)(2,1)S(1)}, u32[]{:S(2)}, u32[]{:S(2)}) collective-permute-start(bf16[128,1024]{1,0:T(8,128)(2,1)S(1)} %get-tuple-element.19), channel_id=1, source_target_pairs={{4,12},{5,13},{10,2},{11,3},{18,26},{19,27},{28,20},{29,21}} | collective-permute-start | bytes 786440 | tf_op jit(solution)/shard_map/ppermute | solution.py:187
  3.4 54.4 %collective-permute-start = (bf16[512,1024]{1,0:T(8,128)(2,1)S(1)}, bf16[512,1024]{1,0:T(8,128)(2,1)}, u32[]{:S(2)}, u32[]{:S(2)}) collective-permute-start(bf16[512,1024]{1,0:T(8,128)(2,1)S(1)} %copy-done), channel_id=1, source_target_pairs={{0,2},{1,3},{14,12},{15,13},{22,20},{23,21},{24,26},{25,27}} | collective-permute-start | bytes 3145736 | tf_op jit(solution)/shard_map/ppermute | solution.py:187
  5.1 54.4 %collective-permute-start.12 = (bf16[512,1024]{1,0:T(8,128)(2,1)S(1)}, bf16[512,1024]{1,0:T(8,128)(2,1)}, u32[]{:S(2)}, u32[]{:S(2)}) collective-permute-start(bf16[512,1024]{1,0:T(8,128)(2,1)S(1)} %copy-done), channel_id=1, source_target_pairs={{6,2},{7,3},{8,12},{9,13},{16,20},{17,21},{30,26},{31,27}} | collective-permute-start | bytes 3145736 | tf_op jit(solution)/shard_map/ppermute | solution.py:187
  11.2 0.8 copy-start.3
  11.2 2.2 %collective-permute-start.5 = (bf16[128,1024]{1,0:T(8,128)(2,1)S(1)}, bf16[128,1024]{1,0:T(8,128)(2,1)S(1)}, u32[]{:S(2)}, u32[]{:S(2)}) collective-permute-start(bf16[128,1024]{1,0:T(8,128)(2,1)S(1)} %get-tuple-element.20), channel_id=1, source_target_pairs={{4,20},{5,21},{10,26},{11,27},{18,2},{19,3},{28,12},{29,13}} | collective-permute-start | bytes 786440 | tf_op jit(solution)/shard_map/ppermute | solution.py:187
  12.1 2.8 %collective-permute-start.17 = (bf16[1032,128]{1,0:T(8,128)(2,1)S(1)}, bf16[1032,128]{1,0:T(8,128)(2,1)S(1)}, u32[]{:S(2)}, u32[]{:S(2)}) collective-permute-start(bf16[1032,128]{1,0:T(8,128)(2,1)S(1)} %shard_map.60.refs_1_), channel_id=1, source_target_pairs={{4,2},{5,3},{10,12},{11,13},{18,20},{19,21},{28,26},{29,27}} | collective-permute-start | bytes 792584 | tf_op jit(solution)/shard_map/ppermute | solution.py:187
  12.8 1.4 %collective-permute-start.3 = (bf16[128,1024]{1,0:T(8,128)(2,1)S(1)}, bf16[128,1024]{1,0:T(8,128)(2,1)S(1)}, u32[]{:S(2)}, u32[]{:S(2)}) collective-permute-start(bf16[128,1024]{1,0:T(8,128)(2,1)S(1)} %get-tuple-element.21), channel_id=1, source_target_pairs={{4,12},{5,13},{10,2},{11,3},{18,26},{19,27},{28,20},{29,21}} | collective-permute-start | bytes 786440 | tf_op jit(solution)/shard_map/ppermute | solution.py:187
  13.5 2.1 %collective-permute-start.10 = (bf16[128,1024]{1,0:T(8,128)(2,1)S(1)}, bf16[128,1024]{1,0:T(8,128)(2,1)S(1)}, u32[]{:S(2)}, u32[]{:S(2)}) collective-permute-start(bf16[128,1024]{1,0:T(8,128)(2,1)S(1)} %collective-permute-done.9), channel_id=1, source_target_pairs={{20,2},{21,3},{26,12},{27,13},{2,20},{3,21},{12,26},{13,27}} | collective-permute-start | bytes 786440 | tf_op jit(solution)/shard_map/ppermute | solution.py:187
  14.1 2.1 %collective-permute-start.8 = (bf16[128,1024]{1,0:T(8,128)(2,1)S(1)}, bf16[128,1024]{1,0:T(8,128)(2,1)S(1)}, u32[]{:S(2)}, u32[]{:S(2)}) collective-permute-start(bf16[128,1024]{1,0:T(8,128)(2,1)S(1)} %collective-permute-done.7), channel_id=1, source_target_pairs={{12,2},{13,3},{2,12},{3,13},{26,20},{27,21},{20,26},{21,27}} | collective-permute-start | bytes 786440 | tf_op jit(solution)/shard_map/ppermute | solution.py:187
  14.8 35.1 %collective-permute-start.6 = (bf16[128,1024]{1,0:T(8,128)(2,1)S(1)}, bf16[128,1024]{1,0:T(8,128)(2,1)S(1)}, u32[]{:S(2)}, u32[]{:S(2)}) collective-permute-start(bf16[128,1024]{1,0:T(8,128)(2,1)S(1)} %collective-permute-done.5), channel_id=1, source_target_pairs={{20,2},{21,3},{26,12},{27,13},{2,20},{3,21},{12,26},{13,27}} | collective-permute-start | bytes 786440 | tf_op jit(solution)/shard_map/ppermute | solution.py:187
  15.5 35.1 %collective-permute-start.4 = (bf16[128,1024]{1,0:T(8,128)(2,1)S(1)}, bf16[128,1024]{1,0:T(8,128)(2,1)S(1)}, u32[]{:S(2)}, u32[]{:S(2)}) collective-permute-start(bf16[128,1024]{1,0:T(8,128)(2,1)S(1)} %collective-permute-done.3), channel_id=1, source_target_pairs={{12,2},{13,3},{2,12},{3,13},{26,20},{27,21},{20,26},{21,27}} | collective-permute-start | bytes 786440 | tf_op jit(solution)/shard_map/ppermute | solution.py:187
  16.2 38.3 %collective-permute-start.15 = (bf16[1032,128]{1,0:T(8,128)(2,1)S(1)}, bf16[1032,128]{1,0:T(8,128)(2,1)S(1)}, u32[]{:S(2)}, u32[]{:S(2)}) collective-permute-start(bf16[1032,128]{1,0:T(8,128)(2,1)S(1)} %shard_map.60.refs_1_), channel_id=1, source_target_pairs={{6,2},{7,3},{8,12},{9,13},{16,20},{17,21},{30,26},{31,27}} | collective-permute-start | bytes 792584 | tf_op jit(solution)/shard_map/ppermute | solution.py:187
  50.0 6.3 %collective-permute-start.14 = (bf16[1032,128]{1,0:T(8,128)(2,1)S(1)}, bf16[1032,128]{1,0:T(8,128)(2,1)S(1)}, u32[]{:S(2)}, u32[]{:S(2)}) collective-permute-start(bf16[1032,128]{1,0:T(8,128)(2,1)S(1)} %shard_map.60.refs_1_), channel_id=1, source_target_pairs={{0,2},{1,3},{14,12},{15,13},{22,20},{23,21},{24,26},{25,27}} | collective-permute-start | bytes 792584 | tf_op jit(solution)/shard_map/ppermute | solution.py:187
  50.7 10.5 %collective-permute-start.18 = (bf16[1032,128]{1,0:T(8,128)(2,1)S(1)}, bf16[1032,128]{1,0:T(8,128)(2,1)S(1)}, u32[]{:S(2)}, u32[]{:S(2)}) collective-permute-start(bf16[1032,128]{1,0:T(8,128)(2,1)S(1)} %collective-permute-done.17.refs_10_), channel_id=1, source_target_pairs={{2,3},{3,2},{12,13},{13,12},{20,21},{21,20},{26,27},{27,26}} | collective-permute-start | bytes 792584 | tf_op jit(solution)/shard_map/ppermute | solution.py:187
  54.6 8.3 %collective-permute-start.2 = (bf16[512,1024]{1,0:T(8,128)(2,1)S(1)}, bf16[512,1024]{1,0:T(8,128)(2,1)}, u32[]{:S(2)}, u32[]{:S(2)}) collective-permute-start(bf16[512,1024]{1,0:T(8,128)(2,1)S(1)} %copy-done), channel_id=1, source_target_pairs={{2,3},{3,2},{12,13},{13,12},{20,21},{21,20},{26,27},{27,26}} | collective-permute-start | bytes 3145736 | tf_op jit(solution)/shard_map/ppermute | solution.py:187
  56.2 6.6 %collective-permute-start.11 = (bf16[512,1024]{1,0:T(8,128)(2,1)S(1)}, bf16[512,1024]{1,0:T(8,128)(2,1)}, u32[]{:S(2)}, u32[]{:S(2)}) collective-permute-start(bf16[512,1024]{1,0:T(8,128)(2,1)S(1)} %shard_map.59.refs_4_), channel_id=1, source_target_pairs={{2,3},{3,2},{12,13},{13,12},{20,21},{21,20},{26,27},{27,26}} | collective-permute-start | bytes 3145736 | tf_op jit(solution)/shard_map/ppermute | solution.py:187
  57.9 5.0 %collective-permute-start.1 = (bf16[512,1024]{1,0:T(8,128)(2,1)}, bf16[512,1024]{1,0:T(8,128)(2,1)}, u32[]{:S(2)}, u32[]{:S(2)}) collective-permute-start(bf16[512,1024]{1,0:T(8,128)(2,1)} %collective-permute-done.refs_0_), channel_id=1, source_target_pairs={{2,3},{3,2},{12,13},{13,12},{20,21},{21,20},{26,27},{27,26}} | collective-permute-start | bytes 3145736 | tf_op jit(solution)/shard_map/ppermute | solution.py:187
  59.5 3.4 %collective-permute-start.13 = (bf16[512,1024]{1,0:T(8,128)(2,1)}, bf16[512,1024]{1,0:T(8,128)(2,1)}, u32[]{:S(2)}, u32[]{:S(2)}) collective-permute-start(bf16[512,1024]{1,0:T(8,128)(2,1)} %collective-permute-done.12.refs_6_), channel_id=1, source_target_pairs={{2,3},{3,2},{12,13},{13,12},{20,21},{21,20},{26,27},{27,26}} | collective-permute-start | bytes 3145736 | tf_op jit(solution)/shard_map/ppermute | solution.py:187
  61.2 1.7 %collective-permute-start.16 = (bf16[3096,128]{1,0:T(8,128)(2,1)S(1)}, bf16[3096,128]{1,0:T(8,128)(2,1)}, u32[]{:S(2)}, u32[]{:S(2)}) collective-permute-start(bf16[3096,128]{1,0:T(8,128)(2,1)S(1)} %shard_map.61.refs_8_), channel_id=1, source_target_pairs={{2,3},{3,2},{12,13},{13,12},{20,21},{21,20},{26,27},{27,26}} | collective-permute-start | bytes 2377736 | tf_op jit(solution)/shard_map/ppermute | solution.py:187
  62.8 36.7 %copy-start.1 = (bf16[1024,128]{1,0:T(8,128)(2,1)S(1)}, bf16[1024,128]{1,0:T(8,128)(2,1)}, u32[]{:S(2)}) copy-start(bf16[1024,128]{1,0:T(8,128)(2,1)} %trial_ref.1) | copy-start | bytes 786436
  73.4 4.0 %collective-permute-start.19 = (bf16[128,512]{1,0:T(8,128)(2,1)S(1)}, bf16[128,512]{1,0:T(8,128)(2,1)S(1)}, u32[]{:S(2)}, u32[]{:S(2)}) collective-permute-start(bf16[128,512]{1,0:T(8,128)(2,1)S(1)} %get-tuple-element.10), channel_id=1, source_target_pairs={{2,0},{3,1},{12,14},{13,15},{20,22},{21,23},{26,24},{27,25}} | collective-permute-start | bytes 393224 | tf_op jit(solution)/shard_map/ppermute | solution.py:187
  74.1 4.0 %collective-permute-start.20 = (bf16[128,512]{1,0:T(8,128)(2,1)S(1)}, bf16[128,512]{1,0:T(8,128)(2,1)S(1)}, u32[]{:S(2)}, u32[]{:S(2)}) collective-permute-start(bf16[128,512]{1,0:T(8,128)(2,1)S(1)} %get-tuple-element.12), channel_id=1, source_target_pairs={{2,4},{3,5},{12,10},{13,11},{20,18},{21,19},{26,28},{27,29}} | collective-permute-start | bytes 393224 | tf_op jit(solution)/shard_map/ppermute | solution.py:187
  74.7 19.2 %collective-permute-start.21 = (bf16[128,512]{1,0:T(8,128)(2,1)S(1)}, bf16[128,512]{1,0:T(8,128)(2,1)S(1)}, u32[]{:S(2)}, u32[]{:S(2)}) collective-permute-start(bf16[128,512]{1,0:T(8,128)(2,1)S(1)} %get-tuple-element.13), channel_id=1, source_target_pairs={{2,6},{3,7},{12,8},{13,9},{20,16},{21,17},{26,30},{27,31}} | collective-permute-start | bytes 393224 | tf_op jit(solution)/shard_map/ppermute | solution.py:187
  76.0 17.9 %collective-permute-start.22 = (bf16[128,512]{1,0:T(8,128)(2,1)S(1)}, bf16[128,512]{1,0:T(8,128)(2,1)S(1)}, u32[]{:S(2)}, u32[]{:S(2)}) collective-permute-start(bf16[128,512]{1,0:T(8,128)(2,1)S(1)} %get-tuple-element.14), channel_id=1, source_target_pairs={{2,1},{3,0},{12,15},{13,14},{20,23},{21,22},{26,25},{27,24}} | collective-permute-start | bytes 393224 | tf_op jit(solution)/shard_map/ppermute | solution.py:187
  76.7 17.2 %collective-permute-start.23 = (bf16[128,512]{1,0:T(8,128)(2,1)S(1)}, bf16[128,512]{1,0:T(8,128)(2,1)S(1)}, u32[]{:S(2)}, u32[]{:S(2)}) collective-permute-start(bf16[128,512]{1,0:T(8,128)(2,1)S(1)} %get-tuple-element.15), channel_id=1, source_target_pairs={{2,3},{3,2},{12,13},{13,12},{20,21},{21,20},{26,27},{27,26}} | collective-permute-start | bytes 393224 | tf_op jit(solution)/shard_map/ppermute | solution.py:187
  77.4 16.5 %collective-permute-start.24 = (bf16[128,512]{1,0:T(8,128)(2,1)S(1)}, bf16[128,512]{1,0:T(8,128)(2,1)S(1)}, u32[]{:S(2)}, u32[]{:S(2)}) collective-permute-start(bf16[128,512]{1,0:T(8,128)(2,1)S(1)} %get-tuple-element.16), channel_id=1, source_target_pairs={{2,5},{3,4},{12,11},{13,10},{20,19},{21,18},{26,29},{27,28}} | collective-permute-start | bytes 393224 | tf_op jit(solution)/shard_map/ppermute | solution.py:187
  78.1 21.5 %collective-permute-start.25 = (bf16[128,512]{1,0:T(8,128)(2,1)S(1)}, bf16[128,512]{1,0:T(8,128)(2,1)S(1)}, u32[]{:S(2)}, u32[]{:S(2)}) collective-permute-start(bf16[128,512]{1,0:T(8,128)(2,1)S(1)} %get-tuple-element.17), channel_id=1, source_target_pairs={{2,7},{3,6},{12,9},{13,8},{20,17},{21,16},{26,31},{27,30}} | collective-permute-start | bytes 393224 | tf_op jit(solution)/shard_map/ppermute | solution.py:187
where the time goes:
time: 102 us; the launch traced here: 101 us
  starting transfers between devices  63.1 us (62%)
  waiting for transfers between devices  23.4 us (23%)
  Pallas kernels  12.1 us (12%)
  local copies, waits for them, and re-layouts  1.4 us (1%)
    ppermute x26, starting transfers between devices, send(): return lax.ppermute(x, AXES, pairs)  63.1 us
    ppermute x26, waiting for transfers between devices, send(): return lax.ppermute(x, AXES, pairs)  23.4 us
    pallas_call x1, Pallas kernels, body(): kernel(functools.partial(root_kernel, plan, spans, width, modes, elems),...  10.5 us
  transfers between devices with their start and end apart: 26, of which 3 were waited for; matrix products, arithmetic and copies ran while one was open for 0% of the time, Pallas kernels for 0%

commit v1 on v0

--- a/solution.py
+++ b/solution.py
@@ -132,17 +132,10 @@
     lax.fori_loop(0, elems, element, 0, unroll=64)
     for c in second:
         c.wait()
-    chunk = p_all.shape[0] // 4
-    for i in range(4):
-        rows = pl.ds(i * chunk, chunk)
-        q_low[rows, :] = q_sum[rows, :].astype(jnp.bfloat16)
-        part = lax.dot_general(
-            p_all[rows, :], q_low[rows, :], (((0,), (0,)), ((), ())), preferred_element_type=jnp.float32
-        )
-        if i == 0:
-            k_acc[...] = part
-        else:
-            k_acc[...] += part
+    q_low[...] = q_sum[...].astype(jnp.bfloat16)
+    k_acc[...] = lax.dot_general(
+        p_all[...], q_low[...], (((0,), (0,)), ((), ())), preferred_element_type=jnp.float32
+    )
     strip = modes // plan.places
     for step in range(chips):
         chip = jnp.where(kind == 1, chips - 1 - step, step)
@@ -153,7 +146,7 @@
 
 def final_kernel(n, where_ref, trial_ref, *refs):
     same, cross = refs[:n], refs[n : 2 * n]
-    k_ref, f_ref, rows = refs[2 * n :]
+    k_ref, f_ref = refs[2 * n :]
     core, step = where_ref[1], where_ref[2]
     half = same[0].shape[1]
     mine = pl.ds(pl.multiple_of(core * half, half), half)
@@ -162,12 +155,12 @@
 
         @pl.when(step == i)
         def _():
-            rows[:, mine] = same[i][...]
-            rows[:, other] = cross[i][...]
-
-    k = rows[...]
-    k_ref[...] = k.astype(jnp.float32)
-    f_ref[...] = jnp.dot(k, trial_ref[...], preferred_element_type=jnp.float32)
+            own, far = same[i][...], cross[i][...]
+            k_ref[:, mine] = own.astype(jnp.float32)
+            k_ref[:, other] = far.astype(jnp.float32)
+            f_ref[...] = jnp.dot(own, trial_ref[mine, :], preferred_element_type=jnp.float32) + jnp.dot(
+                far, trial_ref[other, :], preferred_element_type=jnp.float32
+            )
 
 
 def body(plan, element_tiles, element_blocks, mode_shapes, trial_modes):
@@ -264,7 +257,7 @@
         functools.partial(final_kernel, chips),
         [array((strip, modes), jnp.float32), array((strip, trial_modes.shape[1]), jnp.float32)],
         [SMEM] + [VMEM] * (2 * chips + 1),
-        [pltpu.VMEM((strip, modes), jnp.bfloat16)],
+        [],
         4 << 20,
     )(where, trial_modes, *same, *cross)
 

time: 102 us -> 102 us (level)
  no operation moved by 1% of the time
where the time goes in v1:
time: 102 us; the launch traced here: 101 us
  starting transfers between devices  63.1 us (62%)
  waiting for transfers between devices  23.4 us (23%)
  Pallas kernels  12.2 us (12%)
  local copies, waits for them, and re-layouts  1.4 us (1%)
    ppermute x26, starting transfers between devices, send(): return lax.ppermute(x, AXES, pairs)  63.1 us
    ppermute x26, waiting for transfers between devices, send(): return lax.ppermute(x, AXES, pairs)  23.4 us
    pallas_call x1, Pallas kernels, body(): kernel(functools.partial(root_kernel, plan, spans, width, modes, elems),...  10.5 us
  transfers between devices with their start and end apart: 26, of which 3 were waited for; matrix products, arithmetic and copies ran while one was open for 0% of the time, Pallas kernels for 0%

profile of v1, /device:TPU:3, one launch (start us, length us, event | category | flops | bytes accessed | tf_op | source)
XLA Modules:
  0.0 101.2 jit_solution(7576951768986781127)
XLA Ops:
  0.6 0.0 copy-start
  0.6 0.0 copy-start.2
  0.6 1.4 %fusion = (bf16[128,1024]{1,0:T(8,128)(2,1)S(1)}, bf16[128,1024]{1,0:T(8,128)(2,1)S(1)}, bf16[128,1024]{1,0:T(8,128)(2,1)S(1)}, bf16[128,1024]{1,0:T(8,128)(2,1)S(1)}) fusion(bf16[512,1024]{1,0:T(8,128)(2,1)} %refs_2_.1), kind=kLoop, calls=%fused_computation.1 | loop fusion | bytes 2097152 | tf_op jit(solution)/shard_map/slice | solution.py:204
  2.0 0.7 collective-permute-start.9
  2.7 0.7 collective-permute-start.7
  3.4 0.0 copy-done
  3.4 1.7 %collective-permute-start = (bf16[512,1024]{1,0:T(8,128)(2,1)S(1)}, bf16[512,1024]{1,0:T(8,128)(2,1)}, u32[]{:S(2)}, u32[]{:S(2)}) collective-permute-start(bf16[512,1024]{1,0:T(8,128)(2,1)S(1)} %copy-done), channel_id=1, source_target_pairs={{0,2},{1,3},{14,12},{15,13},{22,20},{23,21},{24,26},{25,27}} | collective-permute-start | bytes 3145736 | tf_op jit(solution)/shard_map/ppermute | solution.py:180
  5.1 6.1 %collective-permute-start.12 = (bf16[512,1024]{1,0:T(8,128)(2,1)S(1)}, bf16[512,1024]{1,0:T(8,128)(2,1)}, u32[]{:S(2)}, u32[]{:S(2)}) collective-permute-start(bf16[512,1024]{1,0:T(8,128)(2,1)S(1)} %copy-done), channel_id=1, source_target_pairs={{6,2},{7,3},{8,12},{9,13},{16,20},{17,21},{30,26},{31,27}} | collective-permute-start | bytes 3145736 | tf_op jit(solution)/shard_map/ppermute | solution.py:180
  11.2 0.8 collective-permute-start.5
  12.0 0.0 copy-done.2
  12.0 0.0 copy-done.3
  12.0 0.0 collective-permute-done.9
  12.1 0.7 collective-permute-start.17
  12.7 0.0 collective-permute-done.7
  12.8 0.7 collective-permute-start.3
  13.4 0.0 collective-permute-done.5
  13.5 0.7 collective-permute-start.10
  14.1 0.0 collective-permute-done.3
  14.1 0.7 collective-permute-start.8
  14.8 0.0 collective-permute-done.17.refs_10_
  14.8 0.7 collective-permute-start.6
  15.5 0.0 collective-permute-done.10.refs_3_
  15.5 0.7 collective-permute-start.4
  16.2 0.0 collective-permute-done.8.refs_2_
  16.2 33.7 %collective-permute-start.15 = (bf16[1032,128]{1,0:T(8,128)(2,1)S(1)}, bf16[1032,128]{1,0:T(8,128)(2,1)S(1)}, u32[]{:S(2)}, u32[]{:S(2)}) collective-permute-start(bf16[1032,128]{1,0:T(8,128)(2,1)S(1)} %shard_map.60.refs_1_), channel_id=1, source_target_pairs={{6,2},{7,3},{8,12},{9,13},{16,20},{17,21},{30,26},{31,27}} | collective-permute-start | bytes 792584 | tf_op jit(solution)/shard_map/ppermute | solution.py:180
  50.0 0.0 collective-permute-done.6.refs_1_
  50.0 0.7 collective-permute-start.14
  50.7 0.0 collective-permute-done.4.refs_0_
  50.7 0.7 collective-permute-start.18
  51.4 0.1 shard_map.59.refs_4_
  51.4 3.2 %collective-permute-done.15.refs_2_ = bf16[1032,128]{1,0:T(8,128)(2,1)S(1)} collective-permute-done((bf16[1032,128]{1,0:T(8,128)(2,1)S(1)}, bf16[1032,128]{1,0:T(8,128)(2,1)S(1)}, u32[]{:S(2)}, u32[]{:S(2)}) %collective-permute-start.15) | collective-permute-done | bytes 264224 | tf_op jit(solution)/shard_map/ppermute | solution.py:180
  54.6 1.7 %collective-permute-start.2 = (bf16[512,1024]{1,0:T(8,128)(2,1)S(1)}, bf16[512,1024]{1,0:T(8,128)(2,1)}, u32[]{:S(2)}, u32[]{:S(2)}) collective-permute-start(bf16[512,1024]{1,0:T(8,128)(2,1)S(1)} %copy-done), channel_id=1, source_target_pairs={{2,3},{3,2},{12,13},{13,12},{20,21},{21,20},{26,27},{27,26}} | collective-permute-start | bytes 3145736 | tf_op jit(solution)/shard_map/ppermute | solution.py:180
  56.2 0.0 collective-permute-done.14.refs_0_
  56.2 1.6 %collective-permute-start.11 = (bf16[512,1024]{1,0:T(8,128)(2,1)S(1)}, bf16[512,1024]{1,0:T(8,128)(2,1)}, u32[]{:S(2)}, u32[]{:S(2)}) collective-permute-start(bf16[512,1024]{1,0:T(8,128)(2,1)S(1)} %shard_map.59.refs_4_), channel_id=1, source_target_pairs={{2,3},{3,2},{12,13},{13,12},{20,21},{21,20},{26,27},{27,26}} | collective-permute-start | bytes 3145736 | tf_op jit(solution)/shard_map/ppermute | solution.py:180
  57.9 0.0 collective-permute-done.refs_0_
  57.9 1.6 %collective-permute-start.1 = (bf16[512,1024]{1,0:T(8,128)(2,1)}, bf16[512,1024]{1,0:T(8,128)(2,1)}, u32[]{:S(2)}, u32[]{:S(2)}) collective-permute-start(bf16[512,1024]{1,0:T(8,128)(2,1)} %collective-permute-done.refs_0_), channel_id=1, source_target_pairs={{2,3},{3,2},{12,13},{13,12},{20,21},{21,20},{26,27},{27,26}} | collective-permute-start | bytes 3145736 | tf_op jit(solution)/shard_map/ppermute | solution.py:180
  59.5 0.0 collective-permute-done.12.refs_6_
  59.5 1.6 %collective-permute-start.13 = (bf16[512,1024]{1,0:T(8,128)(2,1)}, bf16[512,1024]{1,0:T(8,128)(2,1)}, u32[]{:S(2)}, u32[]{:S(2)}) collective-permute-start(bf16[512,1024]{1,0:T(8,128)(2,1)} %collective-permute-done.12.refs_6_), channel_id=1, source_target_pairs={{2,3},{3,2},{12,13},{13,12},{20,21},{21,20},{26,27},{27,26}} | collective-permute-start | bytes 3145736 | tf_op jit(solution)/shard_map/ppermute | solution.py:180
  61.1 0.1 shard_map.61.refs_8_
  61.2 0.0 collective-permute-done.18.refs_11_
  61.2 1.6 %collective-permute-start.16 = (bf16[3096,128]{1,0:T(8,128)(2,1)S(1)}, bf16[3096,128]{1,0:T(8,128)(2,1)}, u32[]{:S(2)}, u32[]{:S(2)}) collective-permute-start(bf16[3096,128]{1,0:T(8,128)(2,1)S(1)} %shard_map.61.refs_8_), channel_id=1, source_target_pairs={{2,3},{3,2},{12,13},{13,12},{20,21},{21,20},{26,27},{27,26}} | collective-permute-start | bytes 2377736 | tf_op jit(solution)/shard_map/ppermute | solution.py:180
  62.8 0.1 pad_add_fusion.where_ref
  62.8 0.0 collective-permute-done.2.refs_3_
  62.9 0.0 collective-permute-done.16.refs_9_
  62.9 0.0 collective-permute-done.11.refs_5_
  62.9 0.0 collective-permute-done.1.refs_1_
  62.9 0.0 collective-permute-done.13.refs_7_
  62.9 10.5 %shard_map.62 = (bf16[128,512]{1,0:T(8,128)(2,1)S(1)}, bf16[128,512]{1,0:T(8,128)(2,1)S(1)}, bf16[128,512]{1,0:T(8,128)(2,1)S(1)}, bf16[128,512]{1,0:T(8,128)(2,...) custom-call(s32[3]{0:T(128)S(1)} %pad_add_fusion.where_ref, ...), custom_call_target="tpu_custom_call" | custom-call | flops 5368709120 | tf_op jit(solution)/shard_map/pallas_call | solution.py:236
  73.4 0.7 collective-permute-start.19
  74.1 0.7 collective-permute-start.20
  74.7 1.3 %collective-permute-start.21 = (bf16[128,512]{1,0:T(8,128)(2,1)S(1)}, bf16[128,512]{1,0:T(8,128)(2,1)S(1)}, u32[]{:S(2)}, u32[]{:S(2)}) collective-permute-start(bf16[128,512]{1,0:T(8,128)(2,1)S(1)} %get-tuple-element.13), channel_id=1, source_target_pairs={{2,6},{3,7},{12,8},{13,9},{20,16},{21,17},{26,30},{27,31}} | collective-permute-start | bytes 393224 | tf_op jit(solution)/shard_map/ppermute | solution.py:180
  76.0 0.7 collective-permute-start.22
  76.7 0.7 collective-permute-start.23
  77.4 0.0 collective-permute-done.19.refs_0_
  77.4 0.7 collective-permute-start.24
  78.1 0.0 collective-permute-done.20.refs_2_
  78.1 1.3 %collective-permute-start.25 = (bf16[128,512]{1,0:T(8,128)(2,1)S(1)}, bf16[128,512]{1,0:T(8,128)(2,1)S(1)}, u32[]{:S(2)}, u32[]{:S(2)}) collective-permute-start(bf16[128,512]{1,0:T(8,128)(2,1)S(1)} %get-tuple-element.17), channel_id=1, source_target_pairs={{2,7},{3,6},{12,9},{13,8},{20,17},{21,16},{26,31},{27,30}} | collective-permute-start | bytes 393224 | tf_op jit(solution)/shard_map/ppermute | solution.py:180
  79.4 14.5 %collective-permute-done.21.refs_3_ = bf16[128,512]{1,0:T(8,128)(2,1)S(1)} collective-permute-done((bf16[128,512]{1,0:T(8,128)(2,1)S(1)}, bf16[128,512]{1,0:T(8,128)(2,1)S(1)}, u32[]{:S(2)}, u32[]{:S(2)}) %collective-permute-start.21) | collective-permute-done | bytes 131104 | tf_op jit(solution)/shard_map/ppermute | solution.py:180
  93.9 0.0 collective-permute-done.22.refs_4_
  93.9 0.0 collective-permute-done.23.refs_5_
  93.9 0.0 collective-permute-done.24.refs_6_
  93.9 5.6 %collective-permute-done.25.refs_7_ = bf16[128,512]{1,0:T(8,128)(2,1)S(1)} collective-permute-done((bf16[128,512]{1,0:T(8,128)(2,1)S(1)}, bf16[128,512]{1,0:T(8,128)(2,1)S(1)}, u32[]{:S(2)}, u32[]{:S(2)}) %collective-permute-start.25) | collective-permute-done | bytes 131104 | tf_op jit(solution)/shard_map/ppermute | solution.py:180
  99.6 0.0 copy-done.1
  99.6 1.6 %shard_map.63 = (f32[128,1024]{1,0:T(8,128)}, f32[128,128]{1,0:T(8,128)}) custom-call(s32[3]{0:T(128)S(1)} %pad_add_fusion.where_ref, bf16[1024,128]{1,0:T(8,128)(2,1)S(1)} %copy-done.1, bf16[128,512]{1,0:T(8,128)(2,1)S(1)} %collective-permute-done.19.refs_0_, bf16[128,512]{1,0:T(8,128)(2,1)S(1)} %get-tuple-element.11.refs_1_, ...), custom_call_target="tpu_custom_call" | custom-call | tf_op jit(solution)/shard_map/pallas_call | solution.py:256
  (3 shorter events, 0.0 us)
Async XLA Ops:
  0.6 2.8 %copy-start = (bf16[512,1024]{1,0:T(8,128)(2,1)S(1)}, bf16[512,1024]{1,0:T(8,128)(2,1)}, u32[]{:S(2)}) copy-start(bf16[512,1024]{1,0:T(8,128)(2,1)} %refs_2_.1) | copy-start | bytes 3145732
  0.6 11.4 %copy-start.2 = (bf16[8,128,128]{2,1,0:T(8,128)(2,1)S(1)}, bf16[8,128,128]{2,1,0:T(8,128)(2,1)}, u32[]{:S(2)}) copy-start(bf16[8,128,128]{2,1,0:T(8,128)(2,1)} %t_ref.1) | copy-start | bytes 786436
  2.0 10.0 %collective-permute-start.9 = (bf16[128,1024]{1,0:T(8,128)(2,1)S(1)}, bf16[128,1024]{1,0:T(8,128)(2,1)S(1)}, u32[]{:S(2)}, u32[]{:S(2)}) collective-permute-start(bf16[128,1024]{1,0:T(8,128)(2,1)S(1)} %get-tuple-element.18), channel_id=1, source_target_pairs={{4,20},{5,21},{10,26},{11,27},{18,2},{19,3},{28,12},{29,13}} | collective-permute-start | bytes 786440 | tf_op jit(solution)/shard_map/ppermute | solution.py:180
  2.7 10.0 %collective-permute-start.7 = (bf16[128,1024]{1,0:T(8,128)(2,1)S(1)}, bf16[128,1024]{1,0:T(8,128)(2,1)S(1)}, u32[]{:S(2)}, u32[]{:S(2)}) collective-permute-start(bf16[128,1024]{1,0:T(8,128)(2,1)S(1)} %get-tuple-element.19), channel_id=1, source_target_pairs={{4,12},{5,13},{10,2},{11,3},{18,26},{19,27},{28,20},{29,21}} | collective-permute-start | bytes 786440 | tf_op jit(solution)/shard_map/ppermute | solution.py:180
  3.4 54.4 %collective-permute-start = (bf16[512,1024]{1,0:T(8,128)(2,1)S(1)}, bf16[512,1024]{1,0:T(8,128)(2,1)}, u32[]{:S(2)}, u32[]{:S(2)}) collective-permute-start(bf16[512,1024]{1,0:T(8,128)(2,1)S(1)} %copy-done), channel_id=1, source_target_pairs={{0,2},{1,3},{14,12},{15,13},{22,20},{23,21},{24,26},{25,27}} | collective-permute-start | bytes 3145736 | tf_op jit(solution)/shard_map/ppermute | solution.py:180
  5.1 54.4 %collective-permute-start.12 = (bf16[512,1024]{1,0:T(8,128)(2,1)S(1)}, bf16[512,1024]{1,0:T(8,128)(2,1)}, u32[]{:S(2)}, u32[]{:S(2)}) collective-permute-start(bf16[512,1024]{1,0:T(8,128)(2,1)S(1)} %copy-done), channel_id=1, source_target_pairs={{6,2},{7,3},{8,12},{9,13},{16,20},{17,21},{30,26},{31,27}} | collective-permute-start | bytes 3145736 | tf_op jit(solution)/shard_map/ppermute | solution.py:180
  11.2 0.8 copy-start.3
  11.2 2.2 %collective-permute-start.5 = (bf16[128,1024]{1,0:T(8,128)(2,1)S(1)}, bf16[128,1024]{1,0:T(8,128)(2,1)S(1)}, u32[]{:S(2)}, u32[]{:S(2)}) collective-permute-start(bf16[128,1024]{1,0:T(8,128)(2,1)S(1)} %get-tuple-element.20), channel_id=1, source_target_pairs={{4,20},{5,21},{10,26},{11,27},{18,2},{19,3},{28,12},{29,13}} | collective-permute-start | bytes 786440 | tf_op jit(solution)/shard_map/ppermute | solution.py:180
  12.1 2.8 %collective-permute-start.17 = (bf16[1032,128]{1,0:T(8,128)(2,1)S(1)}, bf16[1032,128]{1,0:T(8,128)(2,1)S(1)}, u32[]{:S(2)}, u32[]{:S(2)}) collective-permute-start(bf16[1032,128]{1,0:T(8,128)(2,1)S(1)} %shard_map.60.refs_1_), channel_id=1, source_target_pairs={{4,2},{5,3},{10,12},{11,13},{18,20},{19,21},{28,26},{29,27}} | collective-permute-start | bytes 792584 | tf_op jit(solution)/shard_map/ppermute | solution.py:180
  12.8 1.4 %collective-permute-start.3 = (bf16[128,1024]{1,0:T(8,128)(2,1)S(1)}, bf16[128,1024]{1,0:T(8,128)(2,1)S(1)}, u32[]{:S(2)}, u32[]{:S(2)}) collective-permute-start(bf16[128,1024]{1,0:T(8,128)(2,1)S(1)} %get-tuple-element.21), channel_id=1, source_target_pairs={{4,12},{5,13},{10,2},{11,3},{18,26},{19,27},{28,20},{29,21}} | collective-permute-start | bytes 786440 | tf_op jit(solution)/shard_map/ppermute | solution.py:180
  13.5 2.1 %collective-permute-start.10 = (bf16[128,1024]{1,0:T(8,128)(2,1)S(1)}, bf16[128,1024]{1,0:T(8,128)(2,1)S(1)}, u32[]{:S(2)}, u32[]{:S(2)}) collective-permute-start(bf16[128,1024]{1,0:T(8,128)(2,1)S(1)} %collective-permute-done.9), channel_id=1, source_target_pairs={{20,2},{21,3},{26,12},{27,13},{2,20},{3,21},{12,26},{13,27}} | collective-permute-start | bytes 786440 | tf_op jit(solution)/shard_map/ppermute | solution.py:180
  14.1 2.1 %collective-permute-start.8 = (bf16[128,1024]{1,0:T(8,128)(2,1)S(1)}, bf16[128,1024]{1,0:T(8,128)(2,1)S(1)}, u32[]{:S(2)}, u32[]{:S(2)}) collective-permute-start(bf16[128,1024]{1,0:T(8,128)(2,1)S(1)} %collective-permute-done.7), channel_id=1, source_target_pairs={{12,2},{13,3},{2,12},{3,13},{26,20},{27,21},{20,26},{21,27}} | collective-permute-start | bytes 786440 | tf_op jit(solution)/shard_map/ppermute | solution.py:180
  14.8 35.1 %collective-permute-start.6 = (bf16[128,1024]{1,0:T(8,128)(2,1)S(1)}, bf16[128,1024]{1,0:T(8,128)(2,1)S(1)}, u32[]{:S(2)}, u32[]{:S(2)}) collective-permute-start(bf16[128,1024]{1,0:T(8,128)(2,1)S(1)} %collective-permute-done.5), channel_id=1, source_target_pairs={{20,2},{21,3},{26,12},{27,13},{2,20},{3,21},{12,26},{13,27}} | collective-permute-start | bytes 786440 | tf_op jit(solution)/shard_map/ppermute | solution.py:180
  15.5 35.1 %collective-permute-start.4 = (bf16[128,1024]{1,0:T(8,128)(2,1)S(1)}, bf16[128,1024]{1,0:T(8,128)(2,1)S(1)}, u32[]{:S(2)}, u32[]{:S(2)}) collective-permute-start(bf16[128,1024]{1,0:T(8,128)(2,1)S(1)} %collective-permute-done.3), channel_id=1, source_target_pairs={{12,2},{13,3},{2,12},{3,13},{26,20},{27,21},{20,26},{21,27}} | collective-permute-start | bytes 786440 | tf_op jit(solution)/shard_map/ppermute | solution.py:180
  16.2 38.3 %collective-permute-start.15 = (bf16[1032,128]{1,0:T(8,128)(2,1)S(1)}, bf16[1032,128]{1,0:T(8,128)(2,1)S(1)}, u32[]{:S(2)}, u32[]{:S(2)}) collective-permute-start(bf16[1032,128]{1,0:T(8,128)(2,1)S(1)} %shard_map.60.refs_1_), channel_id=1, source_target_pairs={{6,2},{7,3},{8,12},{9,13},{16,20},{17,21},{30,26},{31,27}} | collective-permute-start | bytes 792584 | tf_op jit(solution)/shard_map/ppermute | solution.py:180
  50.0 6.3 %collective-permute-start.14 = (bf16[1032,128]{1,0:T(8,128)(2,1)S(1)}, bf16[1032,128]{1,0:T(8,128)(2,1)S(1)}, u32[]{:S(2)}, u32[]{:S(2)}) collective-permute-start(bf16[1032,128]{1,0:T(8,128)(2,1)S(1)} %shard_map.60.refs_1_), channel_id=1, source_target_pairs={{0,2},{1,3},{14,12},{15,13},{22,20},{23,21},{24,26},{25,27}} | collective-permute-start | bytes 792584 | tf_op jit(solution)/shard_map/ppermute | solution.py:180
  50.7 10.5 %collective-permute-start.18 = (bf16[1032,128]{1,0:T(8,128)(2,1)S(1)}, bf16[1032,128]{1,0:T(8,128)(2,1)S(1)}, u32[]{:S(2)}, u32[]{:S(2)}) collective-permute-start(bf16[1032,128]{1,0:T(8,128)(2,1)S(1)} %collective-permute-done.17.refs_10_), channel_id=1, source_target_pairs={{2,3},{3,2},{12,13},{13,12},{20,21},{21,20},{26,27},{27,26}} | collective-permute-start | bytes 792584 | tf_op jit(solution)/shard_map/ppermute | solution.py:180
  54.6 8.3 %collective-permute-start.2 = (bf16[512,1024]{1,0:T(8,128)(2,1)S(1)}, bf16[512,1024]{1,0:T(8,128)(2,1)}, u32[]{:S(2)}, u32[]{:S(2)}) collective-permute-start(bf16[512,1024]{1,0:T(8,128)(2,1)S(1)} %copy-done), channel_id=1, source_target_pairs={{2,3},{3,2},{12,13},{13,12},{20,21},{21,20},{26,27},{27,26}} | collective-permute-start | bytes 3145736 | tf_op jit(solution)/shard_map/ppermute | solution.py:180
  56.2 6.6 %collective-permute-start.11 = (bf16[512,1024]{1,0:T(8,128)(2,1)S(1)}, bf16[512,1024]{1,0:T(8,128)(2,1)}, u32[]{:S(2)}, u32[]{:S(2)}) collective-permute-start(bf16[512,1024]{1,0:T(8,128)(2,1)S(1)} %shard_map.59.refs_4_), channel_id=1, source_target_pairs={{2,3},{3,2},{12,13},{13,12},{20,21},{21,20},{26,27},{27,26}} | collective-permute-start | bytes 3145736 | tf_op jit(solution)/shard_map/ppermute | solution.py:180
  57.9 5.0 %collective-permute-start.1 = (bf16[512,1024]{1,0:T(8,128)(2,1)}, bf16[512,1024]{1,0:T(8,128)(2,1)}, u32[]{:S(2)}, u32[]{:S(2)}) collective-permute-start(bf16[512,1024]{1,0:T(8,128)(2,1)} %collective-permute-done.refs_0_), channel_id=1, source_target_pairs={{2,3},{3,2},{12,13},{13,12},{20,21},{21,20},{26,27},{27,26}} | collective-permute-start | bytes 3145736 | tf_op jit(solution)/shard_map/ppermute | solution.py:180
  59.5 3.4 %collective-permute-start.13 = (bf16[512,1024]{1,0:T(8,128)(2,1)}, bf16[512,1024]{1,0:T(8,128)(2,1)}, u32[]{:S(2)}, u32[]{:S(2)}) collective-permute-start(bf16[512,1024]{1,0:T(8,128)(2,1)} %collective-permute-done.12.refs_6_), channel_id=1, source_target_pairs={{2,3},{3,2},{12,13},{13,12},{20,21},{21,20},{26,27},{27,26}} | collective-permute-start | bytes 3145736 | tf_op jit(solution)/shard_map/ppermute | solution.py:180
  61.2 1.7 %collective-permute-start.16 = (bf16[3096,128]{1,0:T(8,128)(2,1)S(1)}, bf16[3096,128]{1,0:T(8,128)(2,1)}, u32[]{:S(2)}, u32[]{:S(2)}) collective-permute-start(bf16[3096,128]{1,0:T(8,128)(2,1)S(1)} %shard_map.61.refs_8_), channel_id=1, source_target_pairs={{2,3},{3,2},{12,13},{13,12},{20,21},{21,20},{26,27},{27,26}} | collective-permute-start | bytes 2377736 | tf_op jit(solution)/shard_map/ppermute | solution.py:180
  62.8 36.7 %copy-start.1 = (bf16[1024,128]{1,0:T(8,128)(2,1)S(1)}, bf16[1024,128]{1,0:T(8,128)(2,1)}, u32[]{:S(2)}) copy-start(bf16[1024,128]{1,0:T(8,128)(2,1)} %trial_ref.1) | copy-start | bytes 786436
  73.4 4.0 %collective-permute-start.19 = (bf16[128,512]{1,0:T(8,128)(2,1)S(1)}, bf16[128,512]{1,0:T(8,128)(2,1)S(1)}, u32[]{:S(2)}, u32[]{:S(2)}) collective-permute-start(bf16[128,512]{1,0:T(8,128)(2,1)S(1)} %get-tuple-element.10), channel_id=1, source_target_pairs={{2,0},{3,1},{12,14},{13,15},{20,22},{21,23},{26,24},{27,25}} | collective-permute-start | bytes 393224 | tf_op jit(solution)/shard_map/ppermute | solution.py:180
  74.1 4.0 %collective-permute-start.20 = (bf16[128,512]{1,0:T(8,128)(2,1)S(1)}, bf16[128,512]{1,0:T(8,128)(2,1)S(1)}, u32[]{:S(2)}, u32[]{:S(2)}) collective-permute-start(bf16[128,512]{1,0:T(8,128)(2,1)S(1)} %get-tuple-element.12), channel_id=1, source_target_pairs={{2,4},{3,5},{12,10},{13,11},{20,18},{21,19},{26,28},{27,29}} | collective-permute-start | bytes 393224 | tf_op jit(solution)/shard_map/ppermute | solution.py:180
  74.7 19.2 %collective-permute-start.21 = (bf16[128,512]{1,0:T(8,128)(2,1)S(1)}, bf16[128,512]{1,0:T(8,128)(2,1)S(1)}, u32[]{:S(2)}, u32[]{:S(2)}) collective-permute-start(bf16[128,512]{1,0:T(8,128)(2,1)S(1)} %get-tuple-element.13), channel_id=1, source_target_pairs={{2,6},{3,7},{12,8},{13,9},{20,16},{21,17},{26,30},{27,31}} | collective-permute-start | bytes 393224 | tf_op jit(solution)/shard_map/ppermute | solution.py:180
  76.0 17.9 %collective-permute-start.22 = (bf16[128,512]{1,0:T(8,128)(2,1)S(1)}, bf16[128,512]{1,0:T(8,128)(2,1)S(1)}, u32[]{:S(2)}, u32[]{:S(2)}) collective-permute-start(bf16[128,512]{1,0:T(8,128)(2,1)S(1)} %get-tuple-element.14), channel_id=1, source_target_pairs={{2,1},{3,0},{12,15},{13,14},{20,23},{21,22},{26,25},{27,24}} | collective-permute-start | bytes 393224 | tf_op jit(solution)/shard_map/ppermute | solution.py:180
  76.7 17.2 %collective-permute-start.23 = (bf16[128,512]{1,0:T(8,128)(2,1)S(1)}, bf16[128,512]{1,0:T(8,128)(2,1)S(1)}, u32[]{:S(2)}, u32[]{:S(2)}) collective-permute-start(bf16[128,512]{1,0:T(8,128)(2,1)S(1)} %get-tuple-element.15), channel_id=1, source_target_pairs={{2,3},{3,2},{12,13},{13,12},{20,21},{21,20},{26,27},{27,26}} | collective-permute-start | bytes 393224 | tf_op jit(solution)/shard_map/ppermute | solution.py:180
  77.4 16.5 %collective-permute-start.24 = (bf16[128,512]{1,0:T(8,128)(2,1)S(1)}, bf16[128,512]{1,0:T(8,128)(2,1)S(1)}, u32[]{:S(2)}, u32[]{:S(2)}) collective-permute-start(bf16[128,512]{1,0:T(8,128)(2,1)S(1)} %get-tuple-element.16), channel_id=1, source_target_pairs={{2,5},{3,4},{12,11},{13,10},{20,19},{21,18},{26,29},{27,28}} | collective-permute-start | bytes 393224 | tf_op jit(solution)/shard_map/ppermute | solution.py:180
  78.1 21.5 %collective-permute-start.25 = (bf16[128,512]{1,0:T(8,128)(2,1)S(1)}, bf16[128,512]{1,0:T(8,128)(2,1)S(1)}, u32[]{:S(2)}, u32[]{:S(2)}) collective-permute-start(bf16[128,512]{1,0:T(8,128)(2,1)S(1)} %get-tuple-element.17), channel_id=1, source_target_pairs={{2,7},{3,6},{12,9},{13,8},{20,17},{21,16},{26,31},{27,30}} | collective-permute-start | bytes 393224 | tf_op jit(solution)/shard_map/ppermute | solution.py:180
